TPU v7x, 128 devices: a whole 4x4x4 slice. The times are simulated.
128 devices in a mesh: data: 32 (over z, y, x_hi), width: 4 (over x_lo, core).
Axes of the slice: x: 4 (x_hi: 2, x_lo: 2; x = x_hi * 2 + x_lo), y: 4, z: 4, core: 2. Of those that a mesh axis runs over, the one named last changes fastest.
Arguments:
- grad_up: float32 [32, 768, 3072], P('data', None, 'width'), may hold values from -6 to 6
- grad_down: float32 [32, 3072, 768], P('data', 'width'), may hold values from -6 to 6
- grad_query: float32 [32, 768, 768], P('data', None, 'width'), may hold values from -6 to 6
- grad_key: float32 [32, 768, 768], P('data', None, 'width'), may hold values from -6 to 6
- grad_value: float32 [32, 768, 768], P('data', None, 'width'), may hold values from -6 to 6
- grad_mixed: float32 [32, 768, 768], P('data', 'width'), may hold values from -6 to 6
- grad_norm: float32 [32, 768], P('data'), may hold values from -12 to 12
- weight_up: float32 [768, 3072], P('data', 'width'), may hold values from -0.21875 to 0.21875
- weight_down: float32 [3072, 768], P('width', 'data'), may hold values from -0.109375 to 0.109375
- weight_query: float32 [768, 768], P('data', 'width'), may hold values from -0.21875 to 0.21875
- weight_key: float32 [768, 768], P('data', 'width'), may hold values from -0.21875 to 0.21875
- weight_value: float32 [768, 768], P('data', 'width'), may hold values from -0.21875 to 0.21875
- weight_mixed: float32 [768, 768], P('width', 'data'), may hold values from -0.21875 to 0.21875
- weight_norm: float32 [768], P('data'), may hold values from 0.25 to 1.75
- moment_up: float32 [768, 3072], P('data', 'width'), may hold values from 0.05 to 0.8
- moment_down: float32 [3072, 768], P('width', 'data'), may hold values from 0.05 to 0.8
- moment_query: float32 [768, 768], P('data', 'width'), may hold values from 0.05 to 0.8
- moment_key: float32 [768, 768], P('data', 'width'), may hold values from 0.05 to 0.8
- moment_value: float32 [768, 768], P('data', 'width'), may hold values from 0.05 to 0.8
- moment_mixed: float32 [768, 768], P('width', 'data'), may hold values from 0.05 to 0.8
- moment_norm: float32 [768], P('data'), may hold values from 0.05 to 0.8
Outputs:
- copy_up: bfloat16 [768, 3072], P(None, 'width')
- copy_down: bfloat16 [3072, 768], P('width')
- copy_query: bfloat16 [768, 768], P(None, 'width')
- copy_key: bfloat16 [768, 768], P(None, 'width')
- copy_value: bfloat16 [768, 768], P(None, 'width')
- copy_mixed: bfloat16 [768, 768], P('width')
- copy_norm: bfloat16 [768], replicated
- new_up: float32 [768, 3072], P('data', 'width')
- new_down: float32 [3072, 768], P('width', 'data')
- new_query: float32 [768, 768], P('data', 'width')
- new_key: float32 [768, 768], P('data', 'width')
- new_value: float32 [768, 768], P('data', 'width')
- new_mixed: float32 [768, 768], P('width', 'data')
- new_norm: float32 [768], P('data')
- state_new_up: float32 [768, 3072], P('data', 'width')
- state_new_down: float32 [3072, 768], P('width', 'data')
- state_new_query: float32 [768, 768], P('data', 'width')
- state_new_key: float32 [768, 768], P('data', 'width')
- state_new_value: float32 [768, 768], P('data', 'width')
- state_new_mixed: float32 [768, 768], P('width', 'data')
- state_new_norm: float32 [768], P('data')
All inputs are finite; a program needn't handle non-finite values.
Results may differ from a plain program's by a relative error of at most 0.0004.
Values may be sent and summed in bfloat16 or wider, within the bound.
A program may use at most 128 MiB of HBM per device.

v0:
```python
import jax
import jax.numpy as jnp
from jax import lax
from jax.sharding import PartitionSpec as P

learn_rate = 0.05
hold_rate = 0.9


def in_blocks(x, dim, devices):
    shape = x.shape
    blocks = x.reshape(*shape[:dim], devices, shape[dim] // devices, *shape[dim + 1 :])
    return jnp.moveaxis(blocks, dim, 0)


def one_scatter(arrays, axis, dims):
    devices = lax.axis_size(axis)
    blocks = [in_blocks(a, dim, devices) for a, dim in zip(arrays, dims)]
    lines = jnp.concatenate([b.reshape(devices, -1) for b in blocks], axis=1)
    span = max(16, -(-lines.shape[1] // 1024) * 8)
    lines = jnp.pad(lines, ((0, 0), (0, span * 128 - lines.shape[1]))).reshape(-1, 128)
    line, at, gathered = (lax.psum_scatter(lines, axis, tiled=True).reshape(-1), 0, [])
    for b in blocks:
        part = b[0]
        gathered.append(line[at : at + part.size].reshape(part.shape))
        at += part.size
    return tuple(gathered)


def turned_gather(arrays, axis, dims):
    turned = [jnp.moveaxis(a, dim, 0) for a, dim in zip(arrays, dims)]
    widths = [t[0].size for t in turned]
    both = jnp.concatenate([t.reshape(-1, w) for t, w in zip(turned, widths)], axis=1)
    whole = lax.all_gather(both, axis, axis=0, tiled=True)
    blocks = jnp.split(whole, [sum(widths[:k]) for k in range(1, len(widths))], axis=1)
    return tuple(
        (
            jnp.moveaxis(b.reshape(-1, *t.shape[1:]), 0, dim)
            for b, t, dim in zip(blocks, turned, dims)
        )
    )


def on_device(
    grad_up,
    grad_down,
    grad_query,
    grad_key,
    grad_value,
    grad_mixed,
    grad_norm,
    weight_up,
    weight_down,
    weight_query,
    weight_key,
    weight_value,
    weight_mixed,
    weight_norm,
    moment_up,
    moment_down,
    moment_query,
    moment_key,
    moment_value,
    moment_mixed,
    moment_norm,
):
    mean_up, mean_down, mean_query, mean_key, mean_value, mean_mixed, mean_norm = one_scatter(
        (
            grad_up[0],
            grad_down[0],
            grad_query[0],
            grad_key[0],
            grad_value[0],
            grad_mixed[0],
            grad_norm[0],
        ),
        "data",
        (0, 1, 0, 0, 0, 1, 0),
    )
    mean_rate = lax.axis_size("data") ** (-0.5)
    mean_up = mean_up * mean_rate
    mean_down = mean_down * mean_rate
    mean_query = mean_query * mean_rate
    mean_key = mean_key * mean_rate
    mean_value = mean_value * mean_rate
    mean_mixed = mean_mixed * mean_rate
    mean_norm = mean_norm * mean_rate
    state_new_up = hold_rate * moment_up + (1.0 - hold_rate) * mean_up * mean_up
    new_up = weight_up - learn_rate * mean_up * lax.rsqrt(state_new_up + 1e-06)
    state_new_down = hold_rate * moment_down + (1.0 - hold_rate) * mean_down * mean_down
    new_down = weight_down - learn_rate * mean_down * lax.rsqrt(state_new_down + 1e-06)
    state_new_query = hold_rate * moment_query + (1.0 - hold_rate) * mean_query * mean_query
    new_query = weight_query - learn_rate * mean_query * lax.rsqrt(state_new_query + 1e-06)
    state_new_key = hold_rate * moment_key + (1.0 - hold_rate) * mean_key * mean_key
    new_key = weight_key - learn_rate * mean_key * lax.rsqrt(state_new_key + 1e-06)
    state_new_value = hold_rate * moment_value + (1.0 - hold_rate) * mean_value * mean_value
    new_value = weight_value - learn_rate * mean_value * lax.rsqrt(state_new_value + 1e-06)
    state_new_mixed = hold_rate * moment_mixed + (1.0 - hold_rate) * mean_mixed * mean_mixed
    new_mixed = weight_mixed - learn_rate * mean_mixed * lax.rsqrt(state_new_mixed + 1e-06)
    state_new_norm = hold_rate * moment_norm + (1.0 - hold_rate) * mean_norm * mean_norm
    new_norm = weight_norm - learn_rate * mean_norm * lax.rsqrt(state_new_norm + 1e-06)
    copy_up, copy_down, copy_query, copy_key, copy_value, copy_mixed, copy_norm = turned_gather(
        (
            new_up.astype(jnp.bfloat16),
            new_down.astype(jnp.bfloat16),
            new_query.astype(jnp.bfloat16),
            new_key.astype(jnp.bfloat16),
            new_value.astype(jnp.bfloat16),
            new_mixed.astype(jnp.bfloat16),
            new_norm.astype(jnp.bfloat16),
        ),
        "data",
        (0, 1, 0, 0, 0, 1, 0),
    )
    return (
        copy_up,
        copy_down,
        copy_query,
        copy_key,
        copy_value,
        copy_mixed,
        copy_norm,
        new_up,
        new_down,
        new_query,
        new_key,
        new_value,
        new_mixed,
        new_norm,
        state_new_up,
        state_new_down,
        state_new_query,
        state_new_key,
        state_new_value,
        state_new_mixed,
        state_new_norm,
    )


def solution(mesh):
    return jax.shard_map(
        on_device,
        mesh=mesh,
        in_specs=(
            P("data", None, "width"),
            P("data", "width", None),
            P("data", None, "width"),
            P("data", None, "width"),
            P("data", None, "width"),
            P("data", "width", None),
            P("data", None),
            P("data", "width"),
            P("width", "data"),
            P("data", "width"),
            P("data", "width"),
            P("data", "width"),
            P("width", "data"),
            P("data"),
            P("data", "width"),
            P("width", "data"),
            P("data", "width"),
            P("data", "width"),
            P("data", "width"),
            P("width", "data"),
            P("data"),
        ),
        out_specs=(
            P(None, "width"),
            P("width", None),
            P(None, "width"),
            P(None, "width"),
            P(None, "width"),
            P("width", None),
            P(),
            P("data", "width"),
            P("width", "data"),
            P("data", "width"),
            P("data", "width"),
            P("data", "width"),
            P("width", "data"),
            P("data"),
            P("data", "width"),
            P("width", "data"),
            P("data", "width"),
            P("data", "width"),
            P("data", "width"),
            P("width", "data"),
            P("data"),
        ),
        check_vma=False,
    )
```

profile of v0, /device:TPU:0, one launch (start us, length us, event | category | flops | bytes accessed | tf_op | source)
XLA Modules:
  0.0 577.1 jit_solution(8048873237569944627)
XLA Ops:
  7.2 0.0 all-reduce.4.cloned.1.call-start
  7.2 2.0 copy.97
  9.3 6.6 %copy.98 = f32[32,768,24]{2,1,0:T(8,128)} copy(f32[32,768,24]{1,2,0:T(8,128)S(1)} %bitcast.19) | data formatting | bytes 4718592 | tf_op jit(solution)/shard_map/transpose | solution.py:13
  15.9 11.5 %reshape.120 = f32[32,18432]{1,0:T(8,128)} reshape(f32[32,768,24]{2,1,0:T(8,128)} %copy.98) | data formatting | bytes 4718592 | tf_op jit(solution)/shard_map/reshape | solution.py:19
  27.4 1.9 reshape_reshape_squeeze.12
  29.3 1.6 constant_dynamic-update-slice_fusion.6
  30.9 0.3 copy.99
  31.2 1.1 reshape_reshape_squeeze.13
  32.3 0.3 copy.100
  32.5 1.1 reshape_reshape_squeeze.14
  33.6 1.3 copy.101
  34.9 1.1 reshape_reshape_squeeze.15
  36.1 1.1 copy.102
  37.2 2.0 copy.103
  39.2 3.0 reshape.121
  42.2 0.1 reshape_squeeze.11
  42.3 3.3 constant_dynamic-update-slice_fusion.5
  45.6 2.0 constant_dynamic-update-slice_fusion.4
  47.6 1.9 constant_dynamic-update-slice_fusion.3
  49.6 0.9 constant_dynamic-update-slice_fusion.2
  50.4 0.9 constant_dynamic-update-slice_fusion.1
  51.3 0.6 constant_dynamic-update-slice_fusion
  51.9 6.4 %pad.4 = f32[32,56320]{1,0:T(8,128)} pad(f32[32,55320]{1,0:T(8,128)} %constant_dynamic-update-slice_fusion, f32[]{:T(128)} %constant.15.clone.1), padding=0_0x0_1000 | pad | bytes 14289924 | tf_op jit(solution)/shard_map/jit(_pad)/pad | solution.py:21
  58.3 6.8 %reshape.122 = f32[14080,128]{1,0:T(8,128)} reshape(f32[32,56320]{1,0:T(8,128)} %pad.4) | data formatting | bytes 14417920 | tf_op jit(solution)/shard_map/reshape | solution.py:21
  65.2 0.0 all-reduce.4.cloned.1.call-update
  65.2 0.2 all-gather.2.cloned.1.call-start
  65.4 0.2 copy-done.20
  65.7 0.6 dynamic-slice
  66.9 406.0 %all-reduce.4.cloned.1.call-done = f32[14080,128]{1,0:T(8,128)} async-done(((f32[14080,128]{1,0:T(8,128)}), f32[14080,128]{1,0:T(8,128)}) %all-reduce.4.cloned.1.call-update) | async-done | bytes 7208976
  473.0 0.8 multiply_multiply_fusion.2
  473.8 0.1 mul.238
  473.9 0.1 mul.243
  474.0 0.1 mul.246
  474.0 0.1 mul.251
  474.1 0.1 mul.260
  474.2 0.1 copy.106
  474.3 0.1 mul.254
  474.4 0.1 copy.107
  474.5 0.1 mul.229
  474.5 0.1 mul.235
  474.6 1.0 multiply_multiply_fusion
  475.6 0.2 mul.225
  475.8 0.1 copy.104
  476.0 0.2 mul.219
  476.2 0.1 copy.105
  476.4 1.0 dynamic-slice_bitcast_fusion
  477.4 0.5 convert_bitcast_fusion.2
  477.9 0.1 copy.108
  478.0 0.6 convert_bitcast_fusion.1
  478.6 0.6 fusion.2
  479.3 0.7 convert_bitcast_fusion
  480.0 0.7 fusion.3
  480.7 0.6 fusion
  481.3 0.7 concatenate.7
  482.0 0.0 all-gather.2.cloned.1.call-update
  482.1 76.9 %all-gather.2.cloned.1.call-done = bf16[768,2305]{1,0:T(8,128)(2,1)} async-done(((bf16[24,2305]{1,0:T(8,128)(2,1)}), bf16[768,2305]{1,0:T(8,128)(2,1)}) %all-gather.2.cloned.1.call-update) | async-done | bytes 3540496 | tf_op jit(solution)/shard_map/all_gather | solution.py:34
  559.0 2.8 slice_bitcast_fusion
  561.8 1.4 copy.109
  563.2 1.9 slice_bitcast_fusion.1
  565.1 0.9 copy.110
  566.0 0.9 copy.111
  566.8 0.9 copy.112
  567.7 0.9 copy.113
  568.6 1.7 slice_reduce_fusion
  (44 shorter events, 0.2 us)
Async XLA Ops:
  7.2 465.8 %all-reduce.4.cloned.1.call-start = ((), (), s32[]{:S(2)}) async-start(), calls=%async_computation.1 | async-start | bytes 14417920
  27.4 3.5 copy-start.2
  27.4 4.8 copy-start.3
  30.9 5.1 copy-start.4
  32.3 10.0 %copy-start.17 = (f32[1,768]{1,0:T(1,128)S(1)}, f32[1,768]{1,0:T(1,128)}, u32[]{:S(2)}) copy-start(f32[1,768]{1,0:T(1,128)} %param.27) | copy-start | bytes 9220
  42.2 7.3 %copy-start.1 = (f32[32,4608]{1,0:T(8,128)S(1)}, f32[32,4608]{1,0:T(8,128)}, u32[]{:S(2)}) copy-start(f32[32,4608]{1,0:T(8,128)} %reshape_reshape_squeeze.15) | copy-start | bytes 1769476
  42.2 8.2 %copy-start = (f32[32,4608]{1,0:T(8,128)S(1)}, f32[32,4608]{1,0:T(8,128)}, u32[]{:S(2)}) copy-start(f32[32,4608]{1,0:T(8,128)} %reshape.121) | copy-start | bytes 1769476
  65.0 0.7 copy-start.20
  65.0 412.3 %copy-start.18 = (f32[24]{0:T(128)S(1)}, f32[24]{0:T(128)}, u32[]{:S(2)}) copy-start(f32[24]{0:T(128)} %param.34) | copy-start | bytes 292
  65.0 412.3 %copy-start.19 = (f32[24]{0:T(128)S(1)}, f32[24]{0:T(128)}, u32[]{:S(2)}) copy-start(f32[24]{0:T(128)} %param.41) | copy-start | bytes 292
  65.0 413.0 %copy-start.9 = (f32[192,24]{0,1:T(8,128)S(1)}, f32[192,24]{0,1:T(8,128)}, u32[]{:S(2)}) copy-start(f32[192,24]{0,1:T(8,128)} %param.33) | copy-start | bytes 55300
  65.1 413.0 %copy-start.10 = (f32[192,24]{0,1:T(8,128)S(1)}, f32[192,24]{0,1:T(8,128)}, u32[]{:S(2)}) copy-start(f32[192,24]{0,1:T(8,128)} %param.40) | copy-start | bytes 55300
  65.1 413.6 %copy-start.11 = (f32[24,192]{1,0:T(8,128)S(1)}, f32[24,192]{1,0:T(8,128)}, u32[]{:S(2)}) copy-start(f32[24,192]{1,0:T(8,128)} %param.30) | copy-start | bytes 55300
  65.1 413.6 %copy-start.12 = (f32[24,192]{1,0:T(8,128)S(1)}, f32[24,192]{1,0:T(8,128)}, u32[]{:S(2)}) copy-start(f32[24,192]{1,0:T(8,128)} %param.37) | copy-start | bytes 55300
  65.1 414.2 %copy-start.5 = (f32[768,24]{0,1:T(8,128)S(1)}, f32[768,24]{0,1:T(8,128)}, u32[]{:S(2)}) copy-start(f32[768,24]{0,1:T(8,128)} %param.29) | copy-start | bytes 221188
  65.1 414.2 %copy-start.6 = (f32[768,24]{0,1:T(8,128)S(1)}, f32[768,24]{0,1:T(8,128)}, u32[]{:S(2)}) copy-start(f32[768,24]{0,1:T(8,128)} %param.36) | copy-start | bytes 221188
  65.1 414.8 %copy-start.7 = (f32[24,768]{1,0:T(8,128)S(1)}, f32[24,768]{1,0:T(8,128)}, u32[]{:S(2)}) copy-start(f32[24,768]{1,0:T(8,128)} %param.28) | copy-start | bytes 221188
  65.1 414.8 %copy-start.8 = (f32[24,768]{1,0:T(8,128)S(1)}, f32[24,768]{1,0:T(8,128)}, u32[]{:S(2)}) copy-start(f32[24,768]{1,0:T(8,128)} %param.35) | copy-start | bytes 221188
  65.1 415.5 %copy-start.13 = (f32[24,192]{1,0:T(8,128)S(1)}, f32[24,192]{1,0:T(8,128)}, u32[]{:S(2)}) copy-start(f32[24,192]{1,0:T(8,128)} %param.32) | copy-start | bytes 55300
  65.1 415.5 %copy-start.14 = (f32[24,192]{1,0:T(8,128)S(1)}, f32[24,192]{1,0:T(8,128)}, u32[]{:S(2)}) copy-start(f32[24,192]{1,0:T(8,128)} %param.39) | copy-start | bytes 55300
  65.2 415.5 %copy-start.15 = (f32[24,192]{1,0:T(8,128)S(1)}, f32[24,192]{1,0:T(8,128)}, u32[]{:S(2)}) copy-start(f32[24,192]{1,0:T(8,128)} %param.31) | copy-start | bytes 55300
  65.2 415.5 %copy-start.16 = (f32[24,192]{1,0:T(8,128)S(1)}, f32[24,192]{1,0:T(8,128)}, u32[]{:S(2)}) copy-start(f32[24,192]{1,0:T(8,128)} %param.38) | copy-start | bytes 55300
  65.2 493.8 %all-gather.2.cloned.1.call-start = ((), (), s32[]{:S(2)}) async-start(), calls=%async_computation | async-start | bytes 3852288 | tf_op jit(solution)/shard_map/all_gather | solution.py:34
Sparse Core Ops, SparseCore 0:
  65.3 407.5 all-reduce.3
  482.2 76.7 all-gather.1
where the time goes:
time: 578 us; the launch traced here: 577 us
  waiting for transfers between devices  483 us (84%)
  local copies, waits for them, and re-layouts  73.2 us (13%)
  between operations  15 us (3%)
    unnamed x3, waiting for transfers between devices  406 us
    all_gather x1, waiting for transfers between devices, turned_gather(): whole = lax.all_gather(both, axis, axis=0, tiled=True)  76.9 us
    unnamed x59, local copies, waits for them, and re-layouts  21.4 us
    reshape x2, local copies, waits for them, and re-layouts, one_scatter(): lines = jnp.concatenate([b.reshape(devices, -1) for b in blocks], axis=1)  14.5 us
  transfers between devices with their start and end apart: 2, of which 2 were waited for; matrix products, arithmetic and copies ran while one was open for 0% of the time, Pallas kernels for 0%

commit v1 on v0

--- a/solution.py
+++ b/solution.py
@@ -5,6 +5,16 @@
 
 learn_rate = 0.05
 hold_rate = 0.9
+
+
+def domain_prepare(xx, ax_name):
+    lower = jnp.concatenate(
+        jax.lax.all_to_all(
+            jnp.stack([xx for _ in range(jax.lax.axis_size(ax_name))]), ax_name, 0, 0
+        ),
+        axis=0,
+    )
+    return lower
 
 
 def in_blocks(x, dim, devices):
@@ -31,7 +41,7 @@
     turned = [jnp.moveaxis(a, dim, 0) for a, dim in zip(arrays, dims)]
     widths = [t[0].size for t in turned]
     both = jnp.concatenate([t.reshape(-1, w) for t, w in zip(turned, widths)], axis=1)
-    whole = lax.all_gather(both, axis, axis=0, tiled=True)
+    whole = domain_prepare(both, axis)
     blocks = jnp.split(whole, [sum(widths[:k]) for k in range(1, len(widths))], axis=1)
     return tuple(
         (

time: 578 us -> 534 us (0.924)
  waiting for transfers between devices: 483 us -> 406 us
  blocking collectives: 0 us -> 37.3 us
    all_gather x1 -> x0, waiting for transfers between devices: 76.9 us -> none  [turned_gather(): whole = lax.all_gather(both, axis, axis=0, tiled=True)]
    all_to_all x0 -> x1, blocking collectives: none -> 37.3 us  [domain_prepare(): jax.lax.all_to_all(jnp.stack([xx for _ in range(jax.lax.axis_size(ax_name...]
    unnamed x3 -> x2, waiting for transfers between devices: 406 us -> 406 us
  transfers between devices with their start and end apart: 2 -> 1, of which waited for: 2 -> 1; matrix products, arithmetic and copies ran while one was open for 0% -> 0% of each run, Pallas kernels for 0% -> 0%
where the time goes in v1:
time: 534 us; the launch traced here: 533 us
  waiting for transfers between devices  406 us (76%)
  local copies, waits for them, and re-layouts  69.1 us (13%)
  blocking collectives  37.3 us (7%)
  between operations  15 us (3%)
  other arithmetic  5.58 us (1%)
    unnamed x2, waiting for transfers between devices  406 us
    all_to_all x1, blocking collectives, domain_prepare(): jax.lax.all_to_all(jnp.stack([xx for _ in range(jax.lax.axis_size(ax_name...  37.3 us
    unnamed x59, local copies, waits for them, and re-layouts  21.6 us
    reshape x2, local copies, waits for them, and re-layouts, one_scatter(): lines = jnp.concatenate([b.reshape(devices, -1) for b in blocks], axis=1)  14.5 us
  transfers between devices with their start and end apart: 1, of which 1 were waited for; matrix products, arithmetic and copies ran while one was open for 0% of the time, Pallas kernels for 0%

profile of v1, /device:TPU:0, one launch (start us, length us, event | category | flops | bytes accessed | tf_op | source)
XLA Modules:
  0.0 533.1 jit_solution(16932050893258462736)
XLA Ops:
  7.2 0.0 all-reduce.4.cloned.1.call-start
  7.2 2.0 copy.99
  9.3 6.7 %copy.100 = f32[32,768,24]{2,1,0:T(8,128)} copy(f32[32,768,24]{1,2,0:T(8,128)S(1)} %bitcast.23) | data formatting | bytes 4718592 | tf_op jit(solution)/shard_map/transpose | solution.py:23
  16.0 11.5 %reshape.125 = f32[32,18432]{1,0:T(8,128)} reshape(f32[32,768,24]{2,1,0:T(8,128)} %copy.100) | data formatting | bytes 4718592 | tf_op jit(solution)/shard_map/reshape | solution.py:29
  27.5 1.9 reshape_reshape_squeeze.12
  29.4 1.6 constant_dynamic-update-slice_fusion.6
  31.0 0.3 copy.101
  31.2 1.1 reshape_reshape_squeeze.13
  32.3 0.3 copy.102
  32.6 1.1 reshape_reshape_squeeze.14
  33.7 1.3 copy.103
  35.0 1.1 reshape_reshape_squeeze.15
  36.1 1.1 copy.104
  37.2 2.0 copy.105
  39.3 3.0 reshape.126
  42.3 0.1 reshape_squeeze.11
  42.4 3.3 constant_dynamic-update-slice_fusion.5
  45.7 1.9 constant_dynamic-update-slice_fusion.4
  47.6 1.9 constant_dynamic-update-slice_fusion.3
  49.6 0.9 constant_dynamic-update-slice_fusion.2
  50.4 0.9 constant_dynamic-update-slice_fusion.1
  51.3 0.6 constant_dynamic-update-slice_fusion
  51.9 6.4 %pad.4 = f32[32,56320]{1,0:T(8,128)} pad(f32[32,55320]{1,0:T(8,128)} %constant_dynamic-update-slice_fusion, f32[]{:T(128)} %constant.15.clone.1), padding=0_0x0_1000 | pad | bytes 14289924 | tf_op jit(solution)/shard_map/jit(_pad)/pad | solution.py:31
  58.3 6.8 %reshape.127 = f32[14080,128]{1,0:T(8,128)} reshape(f32[32,56320]{1,0:T(8,128)} %pad.4) | data formatting | bytes 14417920 | tf_op jit(solution)/shard_map/reshape | solution.py:31
  65.1 0.0 copy-start.10
  65.2 0.0 all-reduce.4.cloned.1.call-update
  65.3 0.5 copy-done.20
  65.7 0.6 dynamic-slice
  67.0 406.0 %all-reduce.4.cloned.1.call-done = f32[14080,128]{1,0:T(8,128)} async-done(((f32[14080,128]{1,0:T(8,128)}), f32[14080,128]{1,0:T(8,128)}) %all-reduce.4.cloned.1.call-update) | async-done | bytes 7208976
  473.0 0.8 multiply_multiply_fusion.2
  473.9 0.1 mul.238
  473.9 0.1 mul.243
  474.0 0.1 mul.246
  474.1 0.1 mul.251
  474.2 0.1 mul.260
  474.3 0.1 copy.108
  474.3 0.1 mul.254
  474.4 0.1 copy.109
  474.5 0.1 mul.229
  474.6 0.1 mul.235
  474.7 1.0 multiply_multiply_fusion
  475.6 0.2 mul.225
  475.9 0.1 copy.106
  476.0 0.2 mul.219
  476.3 0.1 copy.107
  476.4 1.0 dynamic-slice_bitcast_fusion
  477.4 0.5 convert_bitcast_fusion.2
  478.0 0.1 copy.110
  478.1 0.6 convert_bitcast_fusion.1
  478.7 0.6 fusion.2
  479.3 0.7 convert_bitcast_fusion
  480.0 0.7 fusion.3
  480.7 0.6 fusion
  481.3 0.1 concatenate.7
  481.4 0.3 stack.2
  481.7 37.3 %all_to_all.5 = bf16[32,24,2305]{2,1,0:T(8,128)(2,1)S(1)} all-to-all(bf16[32,24,2305]{2,1,0:T(8,128)(2,1)S(1)} %stack.2), channel_id=1, replica_groups=mesh['data'=32,'width'=4] {'data'}, dimensions={0} | all-to-all | bytes 7080960 | tf_op jit(solution)/shard_map/all_to_all | solution.py:12
  519.0 1.2 slice_bitcast_fusion
  520.2 0.4 slice_bitcast_fusion.1
  520.6 0.7 slice_reduce_fusion
  521.3 1.4 copy.111
  522.8 0.9 copy.112
  523.6 0.9 copy.113
  524.5 0.9 copy.114
  525.4 0.9 copy.115
  (43 shorter events, 0.2 us)
Async XLA Ops:
  7.2 465.8 %all-reduce.4.cloned.1.call-start = ((), (), s32[]{:S(2)}) async-start(), calls=%async_computation.1 | async-start | bytes 14417920
  27.5 3.5 copy-start.2
  27.5 4.8 copy-start.3
  31.0 5.1 copy-start.4
  32.3 10.0 %copy-start.17 = (f32[1,768]{1,0:T(1,128)S(1)}, f32[1,768]{1,0:T(1,128)}, u32[]{:S(2)}) copy-start(f32[1,768]{1,0:T(1,128)} %param.27) | copy-start | bytes 9220
  42.3 7.3 %copy-start.1 = (f32[32,4608]{1,0:T(8,128)S(1)}, f32[32,4608]{1,0:T(8,128)}, u32[]{:S(2)}) copy-start(f32[32,4608]{1,0:T(8,128)} %reshape_reshape_squeeze.15) | copy-start | bytes 1769476
  42.3 8.2 %copy-start = (f32[32,4608]{1,0:T(8,128)S(1)}, f32[32,4608]{1,0:T(8,128)}, u32[]{:S(2)}) copy-start(f32[32,4608]{1,0:T(8,128)} %reshape.126) | copy-start | bytes 1769476
  65.1 0.7 copy-start.20
  65.1 412.3 %copy-start.18 = (f32[24]{0:T(128)S(1)}, f32[24]{0:T(128)}, u32[]{:S(2)}) copy-start(f32[24]{0:T(128)} %param.34) | copy-start | bytes 292
  65.1 412.3 %copy-start.19 = (f32[24]{0:T(128)S(1)}, f32[24]{0:T(128)}, u32[]{:S(2)}) copy-start(f32[24]{0:T(128)} %param.41) | copy-start | bytes 292
  65.1 413.0 %copy-start.9 = (f32[192,24]{0,1:T(8,128)S(1)}, f32[192,24]{0,1:T(8,128)}, u32[]{:S(2)}) copy-start(f32[192,24]{0,1:T(8,128)} %param.33) | copy-start | bytes 55300
  65.1 413.0 %copy-start.10 = (f32[192,24]{0,1:T(8,128)S(1)}, f32[192,24]{0,1:T(8,128)}, u32[]{:S(2)}) copy-start(f32[192,24]{0,1:T(8,128)} %param.40) | copy-start | bytes 55300
  65.1 413.6 %copy-start.11 = (f32[24,192]{1,0:T(8,128)S(1)}, f32[24,192]{1,0:T(8,128)}, u32[]{:S(2)}) copy-start(f32[24,192]{1,0:T(8,128)} %param.30) | copy-start | bytes 55300
  65.1 413.6 %copy-start.12 = (f32[24,192]{1,0:T(8,128)S(1)}, f32[24,192]{1,0:T(8,128)}, u32[]{:S(2)}) copy-start(f32[24,192]{1,0:T(8,128)} %param.37) | copy-start | bytes 55300
  65.1 414.2 %copy-start.5 = (f32[768,24]{0,1:T(8,128)S(1)}, f32[768,24]{0,1:T(8,128)}, u32[]{:S(2)}) copy-start(f32[768,24]{0,1:T(8,128)} %param.29) | copy-start | bytes 221188
  65.1 414.2 %copy-start.6 = (f32[768,24]{0,1:T(8,128)S(1)}, f32[768,24]{0,1:T(8,128)}, u32[]{:S(2)}) copy-start(f32[768,24]{0,1:T(8,128)} %param.36) | copy-start | bytes 221188
  65.2 414.8 %copy-start.7 = (f32[24,768]{1,0:T(8,128)S(1)}, f32[24,768]{1,0:T(8,128)}, u32[]{:S(2)}) copy-start(f32[24,768]{1,0:T(8,128)} %param.28) | copy-start | bytes 221188
  65.2 414.8 %copy-start.8 = (f32[24,768]{1,0:T(8,128)S(1)}, f32[24,768]{1,0:T(8,128)}, u32[]{:S(2)}) copy-start(f32[24,768]{1,0:T(8,128)} %param.35) | copy-start | bytes 221188
  65.2 415.5 %copy-start.13 = (f32[24,192]{1,0:T(8,128)S(1)}, f32[24,192]{1,0:T(8,128)}, u32[]{:S(2)}) copy-start(f32[24,192]{1,0:T(8,128)} %param.32) | copy-start | bytes 55300
  65.2 415.5 %copy-start.14 = (f32[24,192]{1,0:T(8,128)S(1)}, f32[24,192]{1,0:T(8,128)}, u32[]{:S(2)}) copy-start(f32[24,192]{1,0:T(8,128)} %param.39) | copy-start | bytes 55300
  65.2 415.5 %copy-start.15 = (f32[24,192]{1,0:T(8,128)S(1)}, f32[24,192]{1,0:T(8,128)}, u32[]{:S(2)}) copy-start(f32[24,192]{1,0:T(8,128)} %param.31) | copy-start | bytes 55300
  65.2 415.5 %copy-start.16 = (f32[24,192]{1,0:T(8,128)S(1)}, f32[24,192]{1,0:T(8,128)}, u32[]{:S(2)}) copy-start(f32[24,192]{1,0:T(8,128)} %param.38) | copy-start | bytes 55300
Sparse Core Ops, SparseCore 0:
  65.4 407.6 all-reduce.3
